TPU v7x, 32 devices: a whole 2x2x4 slice. The times are simulated.
32 devices in a mesh: parts: 2 (over y), row: 8 (over z, core), col: 2 (over x), sub: 1.
Axes of the slice: x: 2, y: 2, z: 4, core: 2. Of those that a mesh axis runs over, the one named last changes fastest.
Arguments:
- pair: float32 [192, 96, 128], P(('parts', 'row'), ('col', 'sub')), parts along dimension 0, may hold values from -250 to 250, as said below
- residue_mask: int32 [192], P('parts'), parts along dimension 0, may hold values from 0 to 1, as said below
- tri_norm_gain: float32 [128], replicated, may hold values from 0.25 to 1.75
- tri_in_weight: bfloat16 [128, 4, 128], replicated, may hold values from -0.5 to 0.5
- tri_gate_weight: bfloat16 [128, 128], replicated, may hold values from -0.5 to 0.5
- tri_out_norm_gain: float32 [128], replicated, may hold values from 0.25 to 1.75
- tri_out_weight: bfloat16 [128, 128], replicated, may hold values from -0.5 to 0.5
- att_norm_gain: float32 [128], replicated, may hold values from 0.25 to 1.75
- att_proj_weight: bfloat16 [128, 4, 128], replicated, may hold values from -0.5 to 0.5
- att_bias_weight: bfloat16 [128, 4], replicated, may hold values from -15 to 15
- att_out_weight: bfloat16 [128, 128], replicated, may hold values from -0.5 to 0.5
Outputs:
- pair_out: float32 [192, 96, 128], P(('parts', 'row'), ('col', 'sub')), parts along dimension 0
There are 2 independent parts, one for each index of `parts`. A program takes and returns all parts, laid end to end along the dimension named above; an argument that names none is the same for every part. Nothing has to cross between parts.
Inputs may be any that keep to these rules, and one draw needn't show every extreme that they name: The pair entries are finite. `residue_mask`: 0 on every residue at or above a length of at least 48 and less than 96; below it 1, except some unresolved residues that are 0; residue 0 is always 1.
All inputs are finite; a program needn't handle non-finite values.
Results may differ from a plain program's by a relative error of at most 0.0032.
Values may be sent and summed in bfloat16 or wider, within the bound.
A program may use at most 64 MiB of HBM per device.

v0:
```python
import math

import jax
import jax.numpy as jnp
from jax import lax
from jax.sharding import PartitionSpec as P

epsilon = 1e-05
mask_penalty = 1000000000.0


def norm_last(values_in, gain):
    center = jnp.mean(values_in, axis=-1, keepdims=True)
    centered = values_in - center
    variance = jnp.mean(centered * centered, axis=-1, keepdims=True)
    return centered * lax.rsqrt(variance + epsilon) * gain


def project(normed, weight):
    flat_rows = normed.reshape(-1, normed.shape[-1])
    product = jnp.dot(flat_rows, weight, preferred_element_type=jnp.float32)
    return product.reshape(normed.shape[:-1] + (weight.shape[1],))


def body(
    pair,
    residue_mask,
    tri_norm_gain,
    tri_in_weight,
    tri_gate_weight,
    tri_out_norm_gain,
    tri_out_weight,
    att_norm_gain,
    att_proj_weight,
    att_bias_weight,
    att_out_weight,
):
    rows_here, cols_here, chan_here = pair.shape
    residues = cols_here * lax.axis_size(("col", "sub"))
    row_offset = lax.axis_index("row") * rows_here
    col_offset = lax.axis_index(("col", "sub")) * cols_here
    residue_live = residue_mask.astype(jnp.float32)
    live_rows = lax.dynamic_slice_in_dim(residue_live, row_offset, rows_here)
    live_cols = lax.dynamic_slice_in_dim(residue_live, col_offset, cols_here)
    pair_live = (live_rows[:, None] * live_cols[None, :])[:, :, None]
    tri_normed = norm_last(pair, tri_norm_gain).astype(jnp.bfloat16)
    in_width = tri_in_weight.shape[2]
    projected = project(tri_normed, tri_in_weight.reshape(tri_in_weight.shape[0], -1)).reshape(
        rows_here, cols_here, 4, in_width
    )
    left_factor = (jax.nn.sigmoid(projected[:, :, 0]) * projected[:, :, 1] * pair_live).astype(
        jnp.bfloat16
    )
    right_factor = (jax.nn.sigmoid(projected[:, :, 2]) * projected[:, :, 3] * pair_live).astype(
        jnp.bfloat16
    )
    left_all, right_all = (
        lax.all_gather(left_factor, ("col", "sub"), axis=1, tiled=True),
        lax.all_gather(right_factor, ("col", "sub"), axis=1, tiled=True),
    )
    exchanged = lax.all_to_all(right_all, "row", split_axis=1, concat_axis=0, tiled=True)
    own_rows = lax.dynamic_slice_in_dim(exchanged, col_offset, cols_here, 0)
    tri_sum = jnp.einsum(
        "ikh,jkh->ijh",
        left_all,
        lax.all_gather(own_rows, "row", axis=1, tiled=True),
        preferred_element_type=jnp.float32,
    )
    hidden_normed = norm_last(tri_sum, tri_out_norm_gain).astype(jnp.bfloat16)
    tri_gate = jax.nn.sigmoid(project(tri_normed, tri_gate_weight))
    pair_mid = pair + tri_gate * project(hidden_normed, tri_out_weight)
    att_normed = norm_last(pair_mid, att_norm_gain).astype(jnp.bfloat16)
    head_width = att_proj_weight.shape[2]
    heads_here = att_bias_weight.shape[1]
    head_size = head_width // heads_here
    projected = project(att_normed, att_proj_weight.reshape(att_proj_weight.shape[0], -1)).reshape(
        rows_here, cols_here, 4, head_width
    )
    queries = (projected[:, :, 0] * head_size ** (-0.5)).astype(jnp.bfloat16)
    key_rows = projected[:, :, 1].astype(jnp.bfloat16)
    value_rows = projected[:, :, 2].astype(jnp.bfloat16)
    att_gate = jax.nn.sigmoid(projected[:, :, 3])
    pair_bias = project(att_normed, att_bias_weight).astype(jnp.bfloat16)
    key_all, value_all = (
        lax.all_gather(key_rows, ("col", "sub"), axis=1, tiled=True),
        lax.all_gather(value_rows, ("col", "sub"), axis=1, tiled=True),
    )
    bias_all_rows = lax.all_gather(pair_bias, "row", axis=0, tiled=True)
    bias_panel = lax.all_to_all(
        bias_all_rows, ("col", "sub"), split_axis=0, concat_axis=1, tiled=True
    )
    mask_row = (residue_live - 1.0) * mask_penalty
    head_bias = jnp.transpose(bias_panel.astype(jnp.float32), (2, 0, 1)) + mask_row[None, None, :]
    block_rows = math.gcd(rows_here, max(1, 512 // cols_here))
    blocks = rows_here // block_rows

    def attend(block_items):
        query_block, key_block, value_block = block_items
        scores = (
            jnp.einsum(
                "ijhd,ikhd->ihjk", query_block, key_block, preferred_element_type=jnp.float32
            )
            + head_bias[None]
        )
        row_max = jnp.max(scores, axis=-1, keepdims=True)
        raised = jnp.exp(scores - row_max)
        weights = (raised / jnp.sum(raised, axis=-1, keepdims=True)).astype(jnp.bfloat16)
        return jnp.einsum(
            "ihjk,ikhd->ijhd", weights, value_block, preferred_element_type=jnp.float32
        )

    attended = lax.map(
        attend,
        (
            queries.reshape(blocks, block_rows, cols_here, heads_here, head_size),
            key_all.reshape(blocks, block_rows, residues, heads_here, head_size),
            value_all.reshape(blocks, block_rows, residues, heads_here, head_size),
        ),
    )
    gated = (attended.reshape(rows_here, cols_here, head_width) * att_gate).astype(jnp.bfloat16)
    return pair_mid + project(gated, att_out_weight)


def solution(mesh):
    placed = (
        P(("parts", "row"), ("col", "sub"), None),
        P("parts"),
        P(),
        P(),
        P(),
        P(),
        P(),
        P(),
        P(),
        P(),
        P(),
    )
    return jax.shard_map(
        body,
        mesh=mesh,
        in_specs=placed,
        out_specs=P(("parts", "row"), ("col", "sub"), None),
        check_vma=False,
    )
```

profile of v0, /device:TPU:0, one launch (start us, length us, event | category | flops | bytes accessed | tf_op | source)
XLA Modules:
  0.0 124.3 jit_solution(9761063542724226572)
XLA Ops:
  6.6 0.7 convert_element_type.57
  7.4 1.1 reduce_sum.63
  8.5 1.2 multiply_reduce_fusion.2
  9.8 0.9 copy.78
  11.5 7.5 %all_gather.18 = bf16[12,96,128]{2,1,0:T(8,128)(2,1)S(1)} all-gather(bf16[12,48,128]{2,1,0:T(8,128)(2,1)S(1)} %get-tuple-element.57), channel_id=1, replica_groups=mesh['parts'=2,'row'=8,'col'=2,'sub'=1] {'col','sub'}, dimensions={1}, use_global_device_ids=true | all-gather | bytes 442368 | tf_op jit(solution)/shard_map/all_gather | solution.py:59
  19.1 17.5 %all_to_all.27 = bf16[12,96,128]{2,0,1:T(8,128)(2,1)S(1)} all-to-all(bf16[12,96,128]{2,0,1:T(8,128)(2,1)S(1)} %copy.46), channel_id=1, replica_groups=mesh['parts'=2,'row'=8,'col'=2,'sub'=1] {'row'}, dimensions={1} | all-to-all | bytes 589824 | tf_op jit(solution)/shard_map/all_to_all | solution.py:61
  36.7 0.7 constant_dynamic-slice_fusion
  37.4 6.1 %all_gather.20 = bf16[12,96,128]{2,1,0:T(8,128)(2,1)S(1)} all-gather(bf16[12,48,128]{2,1,0:T(8,128)(2,1)S(1)} %get-tuple-element.56), channel_id=1, replica_groups=mesh['parts'=2,'row'=8,'col'=2,'sub'=1] {'col','sub'}, dimensions={1}, use_global_device_ids=true | all-gather | bytes 442368 | tf_op jit(solution)/shard_map/all_gather | solution.py:58
  43.5 1.2 copy.52
  44.7 0.8 copy.54
  45.5 1.1 fusion.23
  46.6 12.7 %all-gather.4.cloned.1.call-done = bf16[48,96,128]{2,0,1:T(8,128)(2,1)} async-done(((bf16[48,12,128]{2,0,1:T(8,128)(2,1)}), bf16[48,96,128]{2,0,1:T(8,128)(2,1)}) %all-gather.4.cloned.1.call-update) | async-done | bytes 1179664 | tf_op jit(solution)/shard_map/all_gather | solution.py:66
  59.3 5.3 %copy.51 = bf16[48,96,128]{0,1,2:T(8,128)(2,1)S(1)} copy(bf16[48,96,128]{2,0,1:T(8,128)(2,1)} %all-gather.4.cloned.1.call-done) | data formatting | bytes 2359296 | tf_op jit(solution)/shard_map/all_gather | solution.py:66
  64.6 2.0 %fusion.66 = (f32[12,48]{1,0:T(8,128)S(1)}, f32[12,48,128]{1,0,2:T(8,128)S(1)}) fusion(bf16[48,96,128]{0,1,2:T(8,128)(2,1)S(1)} %copy.51, bf16[12,96,128]{1,0,2:T(8,128)(2,1)} %copy.52), kind=kOutput, calls=%fused_computation.89 | convolution fusion | flops 14228928 | bytes 1771776 | tf_op jit(solution)/shard_map/ikh,jkh->ijh/dot_general | solution.py:63
  67.0 0.5 copy-done.4
  68.6 13.9 %all_gather.23 = bf16[96,48,4]{1,2,0:T(4,128)(2,1)S(1)} all-gather(bf16[12,48,4]{1,2,0:T(4,128)(2,1)S(1)} %convolution_convert_fusion), channel_id=1, replica_groups=mesh['parts'=2,'row'=8,'col'=2,'sub'=1] {'row'}, dimensions={0}, use_global_device_ids=true | all-gather | bytes 41472 | tf_op jit(solution)/shard_map/all_gather | solution.py:88
  82.5 0.8 reshape.162
  83.3 3.9 %all-to-all-start.1 = ((bf16[2,2,4608]{2,1,0:T(2,128)(2,1)}), bf16[2,2,4608]{2,1,0:T(2,128)(2,1)}, u32[]{:S(2)}, u32[]{:S(2)}) async-start(bf16[2,2,4608]{2,1,0:T(2,128)(2,1)} %reshape.162), calls=%async_computation.1 | async-start | bytes 73728 | tf_op jit(solution)/shard_map/all_to_all | solution.py:89
  87.6 6.8 %all-gather = bf16[12,96,1,128]{3,1,2,0:T(8,128)(2,1)S(1)} all-gather(bf16[12,48,1,128]{3,1,2,0:T(8,128)(2,1)S(1)} %get-tuple-element.59), channel_id=2, replica_groups=mesh['parts'=2,'row'=8,'col'=2,'sub'=1] {'col','sub'}, dimensions={1}, use_global_device_ids=true | all-gather | bytes 442368 | tf_op jit(solution)/shard_map/all_gather | solution.py:86
  94.4 5.9 %all-gather.1 = bf16[12,96,1,128]{3,1,2,0:T(8,128)(2,1)S(1)} all-gather(bf16[12,48,1,128]{3,1,2,0:T(8,128)(2,1)S(1)} %get-tuple-element.58), channel_id=3, replica_groups=mesh['parts'=2,'row'=8,'col'=2,'sub'=1] {'col','sub'}, dimensions={1}, use_global_device_ids=true | all-gather | bytes 442368 | tf_op jit(solution)/shard_map/all_gather | solution.py:85
  100.3 0.9 copy.55
  101.7 0.9 reshape.163
  103.0 13.3 %while.10 = (s32[]{:T(128)}, f32[6,2,48,4,32]{2,4,3,1,0:T(8,128)S(1)}, bf16[6,2,96,4,32]{2,4,3,1,0:T(8,128)(2,1)}, bf16[6,2,48,4,32]{2,4,3,1,0:T(8,128)(2,1)S(1)...) while((s32[]{:T(128)}, f32[6,2,48,4,32]{2,4,3,1,0:T(8,128)S(1)}, ...), condition=%wide.region_9.10_spmd, body=%wide.region_6.9_spmd.sunk | while | flops 7336512 | bytes 1204813 | solution.py:112
  103.2 0.4 fusion.88
  103.6 1.6 %fusion.89 = f32[6,2,48,4,32]{2,4,3,1,0:T(8,128)S(1)} fusion(f32[6,2,48,4,32]{2,4,3,1,0:T(8,128)S(1)} %get-tuple-element.111, s32[]{:T(128)} %get-tuple-element.110, f32[2,4,48]{2,1,0:T(4,128)S(1)} %fusion.88, bf16[6,2,96,4,32]{2,4,3,1,0:T(8,128)(2,1)} %get-tuple-element.119, f32[2,4,48,96]{3,2,1,0:T(8,128)S(1)} %convolution_add_fusion.3), kind=kOutput, calls=%fused_computation.5.clone.1 | convolution fusion | flops 2470367 | bytes 594944 | tf_op jit(solution)/shard_map/while/body/eval_jaxpr/ihjk,ikhd->ijhd/dot_general | solution.py:108
  105.9 1.6 %fusion.89 = f32[6,2,48,4,32]{2,4,3,1,0:T(8,128)S(1)} fusion(f32[6,2,48,4,32]{2,4,3,1,0:T(8,128)S(1)} %get-tuple-element.111, s32[]{:T(128)} %get-tuple-element.110, f32[2,4,48]{2,1,0:T(4,128)S(1)} %fusion.88, bf16[6,2,96,4,32]{2,4,3,1,0:T(8,128)(2,1)} %get-tuple-element.119, f32[2,4,48,96]{3,2,1,0:T(8,128)S(1)} %convolution_add_fusion.3), kind=kOutput, calls=%fused_computation.5.clone.1 | convolution fusion | flops 2470367 | bytes 594944 | tf_op jit(solution)/shard_map/while/body/eval_jaxpr/ihjk,ikhd->ijhd/dot_general | solution.py:108
  108.1 1.6 %fusion.89 = f32[6,2,48,4,32]{2,4,3,1,0:T(8,128)S(1)} fusion(f32[6,2,48,4,32]{2,4,3,1,0:T(8,128)S(1)} %get-tuple-element.111, s32[]{:T(128)} %get-tuple-element.110, f32[2,4,48]{2,1,0:T(4,128)S(1)} %fusion.88, bf16[6,2,96,4,32]{2,4,3,1,0:T(8,128)(2,1)} %get-tuple-element.119, f32[2,4,48,96]{3,2,1,0:T(8,128)S(1)} %convolution_add_fusion.3), kind=kOutput, calls=%fused_computation.5.clone.1 | convolution fusion | flops 2470367 | bytes 594944 | tf_op jit(solution)/shard_map/while/body/eval_jaxpr/ihjk,ikhd->ijhd/dot_general | solution.py:108
  110.3 1.6 %fusion.89 = f32[6,2,48,4,32]{2,4,3,1,0:T(8,128)S(1)} fusion(f32[6,2,48,4,32]{2,4,3,1,0:T(8,128)S(1)} %get-tuple-element.111, s32[]{:T(128)} %get-tuple-element.110, f32[2,4,48]{2,1,0:T(4,128)S(1)} %fusion.88, bf16[6,2,96,4,32]{2,4,3,1,0:T(8,128)(2,1)} %get-tuple-element.119, f32[2,4,48,96]{3,2,1,0:T(8,128)S(1)} %convolution_add_fusion.3), kind=kOutput, calls=%fused_computation.5.clone.1 | convolution fusion | flops 2470367 | bytes 594944 | tf_op jit(solution)/shard_map/while/body/eval_jaxpr/ihjk,ikhd->ijhd/dot_general | solution.py:108
  112.5 1.6 %fusion.89 = f32[6,2,48,4,32]{2,4,3,1,0:T(8,128)S(1)} fusion(f32[6,2,48,4,32]{2,4,3,1,0:T(8,128)S(1)} %get-tuple-element.111, s32[]{:T(128)} %get-tuple-element.110, f32[2,4,48]{2,1,0:T(4,128)S(1)} %fusion.88, bf16[6,2,96,4,32]{2,4,3,1,0:T(8,128)(2,1)} %get-tuple-element.119, f32[2,4,48,96]{3,2,1,0:T(8,128)S(1)} %convolution_add_fusion.3), kind=kOutput, calls=%fused_computation.5.clone.1 | convolution fusion | flops 2470367 | bytes 594944 | tf_op jit(solution)/shard_map/while/body/eval_jaxpr/ihjk,ikhd->ijhd/dot_general | solution.py:108
  114.3 0.4 fusion.88
  114.7 1.6 %fusion.89 = f32[6,2,48,4,32]{2,4,3,1,0:T(8,128)S(1)} fusion(f32[6,2,48,4,32]{2,4,3,1,0:T(8,128)S(1)} %get-tuple-element.111, s32[]{:T(128)} %get-tuple-element.110, f32[2,4,48]{2,1,0:T(4,128)S(1)} %fusion.88, bf16[6,2,96,4,32]{2,4,3,1,0:T(8,128)(2,1)} %get-tuple-element.119, f32[2,4,48,96]{3,2,1,0:T(8,128)S(1)} %convolution_add_fusion.3), kind=kOutput, calls=%fused_computation.5.clone.1 | convolution fusion | flops 2470367 | bytes 594944 | tf_op jit(solution)/shard_map/while/body/eval_jaxpr/ihjk,ikhd->ijhd/dot_general | solution.py:108
  116.5 0.9 convolution_add_fusion.1
  (71 shorter events, 7.2 us)
Async XLA Ops:
  6.5 60.5 %copy-start = (bf16[128,128]{1,0:T(8,128)(2,1)S(1)}, bf16[128,128]{1,0:T(8,128)(2,1)}, u32[]{:S(2)}) copy-start(bf16[128,128]{1,0:T(8,128)(2,1)} %param.19) | copy-start | bytes 98308
  6.5 4.4 %copy-start.1 = (f32[12,48,128]{2,1,0:T(8,128)S(1)}, f32[12,48,128]{2,1,0:T(8,128)}, u32[]{:S(2)}) copy-start(f32[12,48,128]{2,1,0:T(8,128)} %param.13) | copy-start | bytes 884740
  6.5 4.4 %copy-start.8 = (f32[128]{0:T(128)S(1)}, f32[128]{0:T(128)}, u32[]{:S(2)}) copy-start(f32[128]{0:T(128)} %param.15) | copy-start | bytes 1540
  6.5 52.8 %all-gather.4.cloned.1.call-start = ((), (), s32[]{:S(2)}) async-start(), calls=%async_computation.2 | async-start | bytes 1327104 | tf_op jit(solution)/shard_map/all_gather | solution.py:66
  36.6 8.1 %copy-start.5 = (bf16[128,4,128]{2,1,0:T(4,128)(2,1)S(1)}, bf16[128,4,128]{2,1,0:T(4,128)(2,1)}, u32[]{:S(2)}) copy-start(bf16[128,4,128]{2,1,0:T(4,128)(2,1)} %param.21) | copy-start | bytes 393220
  36.7 8.8 %copy-start.12 = (s32[96]{0:T(128)S(1)}, s32[96]{0:T(128)}, u32[]{:S(2)}) copy-start(s32[96]{0:T(128)} %param.14) | copy-start | bytes 1156
  36.7 8.8 %copy-start.10 = (bf16[128,128]{1,0:T(8,128)(2,1)S(1)}, bf16[128,128]{1,0:T(8,128)(2,1)}, u32[]{:S(2)}) copy-start(bf16[128,128]{1,0:T(8,128)(2,1)} %param.17) | copy-start | bytes 98308
  64.6 2.2 %copy-start.9 = (f32[128]{0:T(128)S(1)}, f32[128]{0:T(128)}, u32[]{:S(2)}) copy-start(f32[128]{0:T(128)} %param.18) | copy-start | bytes 1540
  66.6 1.0 copy-start.4
  67.6 0.7 copy-start.6
  67.6 0.7 copy-start.7
  67.6 19.6 %copy-start.3 = (bf16[512,128]{1,0:T(8,128)(2,1)S(1)}, bf16[512,128]{1,0:T(8,128)(2,1)}, u32[]{:S(2)}) copy-start(bf16[512,128]{1,0:T(8,128)(2,1)} %copy.54) | copy-start | bytes 393220
  83.3 18.4 %all-to-all-start.1 = ((bf16[2,2,4608]{2,1,0:T(2,128)(2,1)}), bf16[2,2,4608]{2,1,0:T(2,128)(2,1)}, u32[]{:S(2)}, u32[]{:S(2)}) async-start(bf16[2,2,4608]{2,1,0:T(2,128)(2,1)} %reshape.162), calls=%async_computation.1 | async-start | bytes 73728 | tf_op jit(solution)/shard_map/all_to_all | solution.py:89
  101.2 1.8 %copy-start.2 = (f32[6,2,48,4,32]{2,4,3,1,0:T(8,128)S(1)}, f32[6,2,48,4,32]{2,4,3,1,0:T(8,128)}, u32[]{:S(2)}) copy-start(f32[6,2,48,4,32]{2,4,3,1,0:T(8,128)} %custom-call) | copy-start | bytes 884740
  103.0 13.6 %copy-start.11 = (bf16[128,128]{1,0:T(8,128)(2,1)S(1)}, bf16[128,128]{1,0:T(8,128)(2,1)}, u32[]{:S(2)}) copy-start(bf16[128,128]{1,0:T(8,128)(2,1)} %param.23) | copy-start | bytes 98308
Sparse Core Ops, SparseCore 0:
  37.5 21.7 all-gather.3
where the time goes:
time: 125 us; the launch traced here: 124 us
  blocking collectives  57.6 us (46%)
  matrix products  18.6 us (15%)
  between operations  13.7 us (11%)
  local copies, waits for them, and re-layouts  13.6 us (11%)
  waiting for transfers between devices  12.8 us (10%)
  other arithmetic  4.1 us (3%)
  starting transfers between devices  3.86 us (3%)
    all_to_all x1, blocking collectives, body(): lax.all_to_all(right_all, 'row', split_axis=1, concat_axis=0, tiled=True)  17.5 us
    all_gather x1, blocking collectives, body(): bias_all_rows = lax.all_gather(pair_bias, 'row', axis=0, tiled=True)  13.9 us
    all_gather x1, waiting for transfers between devices, body(): lax.all_gather(own_rows, 'row', axis=1, tiled=True)  12.7 us
    dot_general x6, matrix products, attend(): jnp.einsum('ihjk,ikhd->ijhd', weights, value_block, preferred_element_typ...  9.36 us
    all_gather x1, blocking collectives, body(): lax.all_gather(right_factor, ('col', 'sub'), axis=1, tiled=True)  7.47 us
    all_gather x1, blocking collectives, body(): lax.all_gather(value_rows, ('col', 'sub'), axis=1, tiled=True)  6.76 us
    all_gather x1, blocking collectives, body(): lax.all_gather(left_factor, ('col', 'sub'), axis=1, tiled=True)  6.06 us
    all_gather x1, blocking collectives, body(): lax.all_gather(key_rows, ('col', 'sub'), axis=1, tiled=True)  5.9 us
  transfers between devices with their start and end apart: 2, of which 1 were waited for; matrix products, arithmetic and copies ran while one was open for 4% of the time, Pallas kernels for 0%

commit v1 on v0

v1 whole, which is shorter than its diff:
```python
import functools
import math

import jax
import jax.numpy as jnp
from jax import lax
from jax.experimental import pallas as pl
from jax.experimental.pallas import tpu as pltpu
from jax.sharding import PartitionSpec as P

epsilon = 1e-05
mask_penalty = 1000000000.0
MESH = pl.DeviceIdType.MESH
F32 = jnp.float32
BF16 = jnp.bfloat16


def norm_last(values_in, gain):
    center = jnp.mean(values_in, axis=-1, keepdims=True)
    centered = values_in - center
    variance = jnp.mean(centered * centered, axis=-1, keepdims=True)
    return centered * lax.rsqrt(variance + epsilon) * gain


def dot(a, b):
    return jnp.dot(a, b, preferred_element_type=F32)


def dot_nt(a, b):
    return lax.dot_general(a, b, (((1,), (1,)), ((), ())), preferred_element_type=F32)


def fold_sublanes(parts):
    lane_row = lax.broadcasted_iota(jnp.int32, parts[0].shape, 0)
    for width in (4, 2, 1):
        low = (lane_row & width) == 0
        half = len(parts) // 2
        folded = []
        for u in range(half):
            x, y = parts[u], parts[u + half]
            if width == 4:
                folded.append(jnp.where(low, x, y) + pltpu.roll(jnp.where(low, y, x), 4, 0))
            else:
                folded.append(
                    jnp.where(low, x, y)
                    + jnp.where(low, pltpu.roll(x, 8 - width, 0), pltpu.roll(y, width, 0))
                )
        parts = folded
    return parts[0]


def kernel(
    dims,
    pair_ref, mask_ref, g1_ref, w_in_ref, w_gate_ref, g2_ref, w_out_ref, g3_ref, w_att_ref, w_bias_ref, w_o_ref,
    out_ref,
    live_s, normed_s, right_all, left_s, gate_s, rf_s, part_s, part_in, sum_s, tri_s, mid_s,
    att_all, q_s, ag_s, k_s, v_s, bias_f, bias_own, bias_all, bfull,
    rs_send, rs_recv, ps_send, ps_recv, as_send, as_recv, bs_send, bs_recv,
):
    nrow, ncol, nsub, group = dims
    rows, cols, chan = pair_ref.shape
    cc = ncol * nsub
    residues = cols * cc
    rb = nrow // cc
    nz = nrow // group
    hid = w_gate_ref.shape[1]
    heads = bias_f.shape[0]
    head_size = hid // heads
    ch = next(n for n in (4, 2, 1) if rows % n == 0)
    nt = rows // ch

    r = lax.axis_index("row")
    c = lax.axis_index("col") * nsub + lax.axis_index("sub")
    z = r // group
    p = r % group

    def at(row, cc_index):
        return {"row": row, "col": cc_index // nsub, "sub": cc_index % nsub}

    barrier = pltpu.get_barrier_semaphore()
    me = r * cc + c

    @pl.loop(1, nrow * cc)
    def _(n):
        other = (me + n) % (nrow * cc)
        pl.semaphore_signal(barrier, inc=1, device_id=at(other // cc, other % cc), device_id_type=MESH)

    live = mask_ref[...].astype(F32)
    eye = lax.broadcasted_iota(jnp.int32, (residues, residues), 0) == lax.broadcasted_iota(
        jnp.int32, (residues, residues), 1
    )
    column = jnp.sum(jnp.where(eye, jnp.broadcast_to(live, (residues, residues)), 0.0), axis=1, keepdims=True)
    live_s[...] = jnp.broadcast_to(column, live_s.shape)
    live_cols = live_s[pl.ds(pl.multiple_of(c * cols, 8), cols), :]

    def right_copy(way, slot, t):
        target = (r + group, r - group, z * group + (group - 1 - p))[way]
        piece = right_all.at[slot, pl.ds(t * ch, ch)]
        return pltpu.make_async_remote_copy(
            src_ref=piece, dst_ref=piece,
            send_sem=rs_send.at[way, slot, t], recv_sem=rs_recv.at[slot, t],
            device_id={"row": target}, device_id_type=MESH,
        )

    for t in range(nt):
        sl = slice(t * ch, (t + 1) * ch)
        normed = norm_last(pair_ref[sl].reshape(ch * cols, chan), g1_ref[...]).astype(BF16)
        normed_s[t] = normed
        proj = dot(normed, w_in_ref[:, 2 * hid :])
        prod = (jax.nn.sigmoid(proj[:, :hid]) * proj[:, hid:]).reshape(ch, cols, hid)
        for u in range(ch):
            both = live_cols * live_s[pl.ds(r * rows + t * ch + u, 1), :]
            right_all[r, t * ch + u] = (prod[u] * both).astype(BF16)
        if t == 0:
            pl.semaphore_wait(barrier, nrow * cc - 1)

        @pl.when(z + 1 < nz)
        def _():
            right_copy(0, r, t).start()

        @pl.when(z >= 1)
        def _():
            right_copy(1, r, t).start()

        if group == 2:
            right_copy(2, r, t).start()

    for t in range(nt):
        proj = dot(normed_s[t], w_in_ref[:, : 2 * hid])
        prod = (jax.nn.sigmoid(proj[:, :hid]) * proj[:, hid:]).reshape(ch, cols, hid)
        gate_s[t] = jax.nn.sigmoid(dot(normed_s[t], w_gate_ref[...]))
        for u in range(ch):
            both = live_cols * live_s[pl.ds(r * rows + t * ch + u, 1), :]
            left_s[t * ch + u] = (prod[u] * both).astype(BF16).astype(F32)

    ig = next(n for n in range(1, 9) if (n * rows) % 8 == 0 and rows % n == 0)

    def part_copy(slot):
        return pltpu.make_async_remote_copy(
            src_ref=part_s.at[slot], dst_ref=part_in.at[c, slot % rb],
            send_sem=ps_send.at[slot], recv_sem=ps_recv.at[c, slot % rb],
            device_id=at(r, slot // rb), device_id_type=MESH,
        )

    def compute(slot):
        rf_s[...] = right_all[slot].astype(F32)

        @pl.loop(0, rows // ig)
        def _(ip):
            accs = [None] * (ig * rows)
            for kv in range(cols // 8):
                ks = slice(kv * 8, kv * 8 + 8)
                lefts = [left_s[ip * ig + u, ks, :] for u in range(ig)]
                for j in range(rows):
                    rv = rf_s[j, ks, :]
                    for u in range(ig):
                        n = u * rows + j
                        term = lefts[u] * rv
                        accs[n] = term if accs[n] is None else accs[n] + term
            for n in range(ig * rows // 8):
                start = pl.multiple_of(ip * (ig * rows) + n * 8, 8)
                part_s[slot, pl.ds(start, 8), :] = fold_sublanes(accs[n * 8 : n * 8 + 8])

        @pl.when(slot // rb != c)
        def _():
            part_copy(slot).start()

    def event(n):
        away = (n + 1) // 2
        return jnp.where(n % 2 == 1, z - away, z + away)

    @pl.loop(1, 2 * nz)
    def _(n):
        zn = event(n)

        @pl.when((zn >= 0) & (zn < nz))
        def _():
            slot = zn * group + p
            for t in range(nt):
                right_copy(0, slot, t).wait_recv()

                @pl.when((zn < z) & (z + 1 < nz))
                def _():
                    right_copy(0, slot, t).start()

                @pl.when((zn > z) & (z >= 1))
                def _():
                    right_copy(1, slot, t).start()

                if group == 2:
                    right_copy(2, slot, t).start()

        zp = event(n - 1)

        @pl.when((zp >= 0) & (zp < nz))
        def _():
            @pl.loop(0, group)
            def _(q):
                slot = zp * group + (p + q) % group

                @pl.when(q == 1)
                def _():
                    for t in range(nt):
                        right_copy(2, slot, t).wait_recv()

                compute(slot)

    for b in range(rb):
        total = part_s[c * rb + b]
        for away in range(1, cc):
            source = (c + away) % cc
            pltpu.make_async_remote_copy(
                src_ref=part_s.at[0], dst_ref=part_in.at[source, b],
                send_sem=ps_send.at[0], recv_sem=ps_recv.at[source, b],
                device_id=at(r, source), device_id_type=MESH,
            ).wait_recv()
            total = total + part_in[source, b]
        sum_s[b] = total
        for i in range(rows):
            tri_s[i, b * rows : (b + 1) * rows, :] = sum_s[b, i * rows : (i + 1) * rows, :]

    def att_copy(t, away, source):
        piece = att_all.at[source, pl.ds(t * ch, ch)]
        return pltpu.make_async_remote_copy(
            src_ref=piece, dst_ref=piece,
            send_sem=as_send.at[away, t], recv_sem=as_recv.at[source, t],
            device_id=at(r, (c + away) % cc), device_id_type=MESH,
        )

    bias_f[...] = jnp.zeros_like(bias_f)
    for t in range(nt):
        sl = slice(t * ch, (t + 1) * ch)
        hidden = norm_last(tri_s[sl].reshape(ch * cols, hid), g2_ref[...]).astype(BF16)
        mid = pair_ref[sl].reshape(ch * cols, chan) + gate_s[t] * dot(hidden, w_out_ref[...])
        mid_s[t] = mid
        att = norm_last(mid, g3_ref[...]).astype(BF16)
        att_all[c, sl] = att.reshape(ch, cols, chan)
        for away in range(1, cc):
            att_copy(t, away, c).start()
        for u in range(ch):
            heads_first = dot_nt(w_bias_ref[...], att[u * cols : (u + 1) * cols])
            for h in range(heads):
                bias_f[h, t * ch + u : t * ch + u + 1, :] = heads_first[h : h + 1, :]

    bias_own[...] = bias_f[...].astype(BF16)
    panel = r // rb

    def bias_copy(row, source_c, source_b):
        return pltpu.make_async_remote_copy(
            src_ref=bias_own, dst_ref=bias_all.at[source_c, source_b],
            send_sem=bs_send.at[row], recv_sem=bs_recv.at[source_c, source_b],
            device_id=at(row, panel), device_id_type=MESH,
        )

    @pl.loop(0, nrow)
    def _(n):
        row = (r + n) % nrow

        @pl.when((n > 0) | (panel != c))
        def _():
            bias_copy(row, c, r % rb).start()

    @pl.when(panel == c)
    def _():
        bias_all[c, r % rb] = bias_f[...].astype(BF16)

    for t in range(nt):
        sl = slice(t * ch, (t + 1) * ch)
        att = att_all[c, sl].reshape(ch * cols, chan)
        proj = dot(att, w_att_ref[...])
        q_s[sl] = (proj[:, :hid] * head_size ** (-0.5)).astype(BF16).reshape(ch, cols, hid)
        k_s[c, sl] = proj[:, hid : 2 * hid].astype(BF16).reshape(ch, cols, hid)
        v_s[c, sl] = proj[:, 2 * hid : 3 * hid].astype(BF16).reshape(ch, cols, hid)
        ag_s[sl] = jax.nn.sigmoid(proj[:, 3 * hid :]).reshape(ch, cols, hid)

    for away in range(1, cc):
        source = (c + away) % cc
        for t in range(nt):
            sl = slice(t * ch, (t + 1) * ch)
            att_copy(t, away, source).wait_recv()
            att = att_all[source, sl].reshape(ch * cols, chan)
            proj = dot(att, w_att_ref[:, hid : 3 * hid])
            k_s[source, sl] = proj[:, :hid].astype(BF16).reshape(ch, cols, hid)
            v_s[source, sl] = proj[:, hid:].astype(BF16).reshape(ch, cols, hid)

    mask_row = (live - 1.0) * mask_penalty
    for source in range(cc):
        for b in range(rb):
            @pl.when((c != source) | (r != c * rb + b))
            def _():
                bias_copy(r, source, b).wait_recv()

            for h in range(heads):
                bfull[h, b * rows : (b + 1) * rows, source * cols : (source + 1) * cols] = (
                    bias_all[source, b, h].astype(F32)[:rows] + mask_row[:, source * cols : (source + 1) * cols]
                )

    head_of = lax.broadcasted_iota(jnp.int32, (cols, hid), 1) // head_size
    ones = jnp.ones((residues, hid), BF16)

    @pl.loop(0, nt)
    def _(t):
        gated = []
        for u in range(ch):
            i = t * ch + u
            query = q_s[i]
            stacked = jnp.concatenate(
                [jnp.where(head_of == h, query, jnp.zeros_like(query)) for h in range(heads)], axis=0
            )
            keys = jnp.concatenate([k_s[s, i] for s in range(cc)], axis=0)
            values = jnp.concatenate([v_s[s, i] for s in range(cc)], axis=0)
            scores = dot_nt(stacked, keys) + bfull[...].reshape(heads * cols, residues)
            raised = jnp.exp(scores - jnp.max(scores, axis=-1, keepdims=True)).astype(BF16)
            both = dot(raised, jnp.concatenate([values, ones], axis=1))
            top, bottom = both[:cols, :hid], both[:cols, hid:]
            for h in range(1, heads):
                rows_h = both[h * cols : (h + 1) * cols]
                top = jnp.where(head_of == h, rows_h[:, :hid], top)
                bottom = jnp.where(head_of == h, rows_h[:, hid:], bottom)
            gated.append((top / bottom * ag_s[i]).astype(BF16))
        result = mid_s[t] + dot(jnp.concatenate(gated, axis=0), w_o_ref[...])
        out_ref[pl.ds(t * ch, ch)] = result.reshape(ch, cols, chan)

    @pl.loop(0, nrow)
    def _(slot):
        zn, pn = slot // group, slot % group

        @pl.when(pn == p)
        def _():
            for t in range(nt):
                @pl.when((zn <= z) & (z + 1 < nz))
                def _():
                    right_copy(0, slot, t).wait_send()

                @pl.when((zn >= z) & (z >= 1))
                def _():
                    right_copy(1, slot, t).wait_send()

                if group == 2:
                    right_copy(2, slot, t).wait_send()

        @pl.when(slot // rb != c)
        def _():
            part_copy(slot).wait_send()

        @pl.when((slot != r) | (panel != c))
        def _():
            bias_copy(slot, c, r % rb).wait_send()

    for away in range(1, cc):
        for t in range(nt):
            att_copy(t, away, c).wait_send()


def body(dims, pair, residue_mask, g1, w_in, w_gate, g2, w_out, g3, w_att, w_bias, w_o):
    nrow, ncol, nsub, group = dims
    rows, cols, chan = pair.shape
    cc = ncol * nsub
    residues = cols * cc
    rb = nrow // cc
    hid = w_in.shape[2]
    heads = w_bias.shape[1]
    ch = next(n for n in (4, 2, 1) if rows % n == 0)
    nt = rows // ch
    pad = -(-rows // 16) * 16
    bias_rows = jnp.pad(w_bias.T, ((0, -heads % 16), (0, 0)))
    V = pltpu.VMEM
    DMA = pltpu.SemaphoreType.DMA
    return pl.pallas_call(
        functools.partial(kernel, dims),
        out_shape=jax.ShapeDtypeStruct(pair.shape, F32),
        in_specs=[pl.BlockSpec(memory_space=pltpu.VMEM)] * 11,
        out_specs=pl.BlockSpec(memory_space=pltpu.VMEM),
        scratch_shapes=[
            V((residues, hid), F32),
            V((nt, ch * cols, chan), BF16),
            V((nrow, rows, cols, hid), BF16),
            V((rows, cols, hid), F32),
            V((nt, ch * cols, chan), F32),
            V((rows, cols, hid), F32),
            V((nrow, rows * rows, hid), F32),
            V((cc, rb, rows * rows, hid), F32),
            V((rb, rows * rows, hid), F32),
            V((rows, cols, hid), F32),
            V((nt, ch * cols, chan), F32),
            V((cc, rows, cols, chan), BF16),
            V((rows, cols, hid), BF16),
            V((rows, cols, hid), F32),
            V((cc, rows, cols, hid), BF16),
            V((cc, rows, cols, hid), BF16),
            V((heads, pad, cols), F32),
            V((heads, pad, cols), BF16),
            V((cc, rb, heads, pad, cols), BF16),
            V((heads, cols, residues), F32),
            DMA((3, nrow, nt)),
            DMA((nrow, nt)),
            DMA((nrow,)),
            DMA((cc, rb)),
            DMA((cc, nt)),
            DMA((cc, nt)),
            DMA((nrow,)),
            DMA((cc, rb)),
        ],
        compiler_params=pltpu.CompilerParams(
            collective_id=0, has_side_effects=True, vmem_limit_bytes=56 * 1024 * 1024
        ),
        name="pair_update",
    )(
        pair,
        residue_mask.reshape(1, -1),
        g1.reshape(1, -1),
        w_in.reshape(chan, -1),
        w_gate,
        g2.reshape(1, -1),
        w_out,
        g3.reshape(1, -1),
        w_att.reshape(chan, -1),
        bias_rows,
        w_o,
    )


def solution(mesh):
    shape = mesh.shape
    group = 2 if shape["sub"] == 1 and shape["row"] % 2 == 0 else 1
    dims = (shape["row"], shape["col"], shape["sub"], group)
    placed = (P(("parts", "row"), ("col", "sub"), None), P("parts")) + (P(),) * 9
    return jax.shard_map(
        functools.partial(body, dims),
        mesh=mesh,
        in_specs=placed,
        out_specs=P(("parts", "row"), ("col", "sub"), None),
        check_vma=False,
    )
```

time: 125 us -> 43.6 us (0.35)
  blocking collectives: 57.6 us -> 0 us
  Pallas kernels: 0 us -> 38.8 us
  matrix products: 18.6 us -> 0 us
  between operations: 13.7 us -> 0.01 us
  waiting for transfers between devices: 12.8 us -> 0 us
  local copies, waits for them, and re-layouts: 13.6 us -> 4.65 us
  other arithmetic: 4.1 us -> 0 us
  starting transfers between devices: 3.86 us -> 0 us
    all_gather x5 -> x0, blocking collectives: 40.1 us -> none  [the longest x1 13.9 us: body(): bias_all_rows = lax.all_gather(pair_bias, 'row', axis=0, tiled=True)]
    pallas_call x0 -> x1, Pallas kernels: none -> 38.8 us  [body(): pl.pallas_call(functools.partial(kernel, dims), out_shape=jax.ShapeDtypeS...]
    all_to_all x1 -> x0, blocking collectives: 17.5 us -> none  [body(): lax.all_to_all(right_all, 'row', split_axis=1, concat_axis=0, tiled=True)]
    dot_general x19 -> x0, matrix products: 16.1 us -> none  [the longest x6 9.36 us: attend(): jnp.einsum('ihjk,ikhd->ijhd', weights, value_block, preferred_element_typ...]
    all_gather x1 -> x0, waiting for transfers between devices: 12.7 us -> none  [body(): lax.all_gather(own_rows, 'row', axis=1, tiled=True)]
    all_gather x5 -> x0, local copies, waits for them, and re-layouts: 7.78 us -> none  [the longest x1 5.29 us: body(): lax.all_gather(own_rows, 'row', axis=1, tiled=True)]
    all_to_all x1 -> x0, starting transfers between devices: 3.86 us -> none  [body(): lax.all_to_all(bias_all_rows, ('col', 'sub'), split_axis=0, concat_axis=1...]
    reduce_sum x4 -> x0, other arithmetic: 2.82 us -> none  [the longest x3 1.71 us: norm_last(): variance = jnp.mean(centered * centered, axis=-1, keepdims=True)]
  transfers between devices with their start and end apart: 2 -> 0, of which waited for: 1 -> 0; matrix products, arithmetic and copies ran while one was open for 4% -> 0% of each run, Pallas kernels for 0% -> 0%
where the time goes in v1:
time: 43.6 us; the launch traced here: 43.4 us
  Pallas kernels  38.8 us (89%)
  local copies, waits for them, and re-layouts  4.65 us (11%)
    pallas_call x1, Pallas kernels, body(): pl.pallas_call(functools.partial(kernel, dims), out_shape=jax.ShapeDtypeS...  38.8 us
    unnamed x3, local copies, waits for them, and re-layouts  2.37 us
    reshape x1, local copies, waits for them, and re-layouts, body(): w_att.reshape(chan, -1)  1.69 us

profile of v1, /device:TPU:0, one launch (start us, length us, event | category | flops | bytes accessed | tf_op | source)
XLA Modules:
  0.0 43.4 jit_solution(17501612014053057858)
XLA Ops:
  0.0 0.0 copy-start
  0.0 0.7 %copy-done = bf16[128,4]{0,1:T(4,128)(2,1)S(1)} copy-done((bf16[128,4]{0,1:T(4,128)(2,1)S(1)}, bf16[128,4]{0,1:T(4,128)(2,1)}, u32[]{:S(2)}) %copy-start) | copy-done | bytes 1048
  0.7 0.6 %pad.4.w_bias_ref = bf16[16,128]{1,0:T(8,128)(2,1)} pad(bf16[4,128]{1,0:T(4,128)(2,1)S(1)} %bitcast.13, bf16[]{:T(256)} %constant.2.clone.1), padding=0_12x0_0 | pad | bytes 5122 | tf_op jit(solution)/shard_map/jit(_pad)/pad | solution.py:366
  1.3 1.7 %copy_bitcast_fusion = (bf16[128,512]{1,0:T(8,128)(2,1)}, bf16[128,512]{1,0:T(8,128)(2,1)}) fusion(bf16[16,8,4,128]{3,2,1,0:T(4,128)(2,1)} %bitcast.11, bf16[16,8,4,128]{3,2,1,0:T(4,128)(2,1)} %bitcast.12), kind=kLoop, calls=%fused_computation | loop fusion | bytes 524288 | tf_op jit(solution)/shard_map/reshape | solution.py:417
  3.0 38.8 %pair_update.1 = f32[12,48,128]{2,1,0:T(8,128)} custom-call(f32[12,48,128]{2,1,0:T(8,128)} %pair_ref.1, s32[1,96]{1,0:T(1,128)} %bitcast.14, f32[1,128]{1,0:T(1,128)} %bitcast.15, bf16[128,512]{1,0:T(8,128)(2,1)} %get-tuple-element.6.w_in_ref, bf16[128,128]{1,0:T(8,128)(2,1)} %w_gate_ref.1, f32[1,128]{1,0:T(1,128)} %bitcast.16, bf16[128,128]{1,0:T(8,128)(2,1)} %w_out_ref.1, ...), custom_call_target="tpu_custom_call" | custom-call | tf_op jit(solution)/shard_map/pair_update/pallas_call | solution.py:369
  41.8 1.7 %copy.17 = f32[12,48,128]{2,1,0:T(8,128)} copy(f32[12,48,128]{2,1,0:T(8,128)} %pair_update.1) | data formatting | bytes 589824
Async XLA Ops:
  0.0 0.7 %copy-start = (bf16[128,4]{0,1:T(4,128)(2,1)S(1)}, bf16[128,4]{0,1:T(4,128)(2,1)}, u32[]{:S(2)}) copy-start(bf16[128,4]{0,1:T(4,128)(2,1)} %param.20) | copy-start | bytes 3076

commit v2 on v1

--- a/solution.py
+++ b/solution.py
@@ -55,7 +55,7 @@
     out_ref,
     live_s, normed_s, right_all, left_s, gate_s, rf_s, part_s, part_in, sum_s, tri_s, mid_s,
     att_all, q_s, ag_s, k_s, v_s, bias_f, bias_own, bias_all, bfull,
-    rs_send, rs_recv, ps_send, ps_recv, as_send, as_recv, bs_send, bs_recv,
+    rs_send, rs_recv, ps_send, ps_recv, as_send, as_recv, bs_send, bs_recv, bf_send,
 ):
     nrow, ncol, nsub, group = dims
     rows, cols, chan = pair_ref.shape
@@ -64,7 +64,7 @@
     rb = nrow // cc
     nz = nrow // group
     hid = w_gate_ref.shape[1]
-    heads = bias_f.shape[0]
+    heads = bias_f.shape[0] * 2
     head_size = hid // heads
     ch = next(n for n in (4, 2, 1) if rows % n == 0)
     nt = rows // ch
@@ -133,91 +133,102 @@
             both = live_cols * live_s[pl.ds(r * rows + t * ch + u, 1), :]
             left_s[t * ch + u] = (prod[u] * both).astype(BF16).astype(F32)
 
-    ig = next(n for n in range(1, 9) if (n * rows) % 8 == 0 and rows % n == 0)
-
-    def part_copy(slot):
+    def part_copy(slot, t):
         return pltpu.make_async_remote_copy(
-            src_ref=part_s.at[slot], dst_ref=part_in.at[c, slot % rb],
-            send_sem=ps_send.at[slot], recv_sem=ps_recv.at[c, slot % rb],
+            src_ref=part_s.at[slot, t], dst_ref=part_in.at[c, slot % rb, t],
+            send_sem=ps_send.at[slot, t], recv_sem=ps_recv.at[c, slot % rb, t],
             device_id=at(r, slot // rb), device_id_type=MESH,
         )
 
-    def compute(slot):
-        rf_s[...] = right_all[slot].astype(F32)
+    ig = next(n for n in (4, 2, 1) if rows % n == 0 and n * ch % 8 == 0)
+
+    def compute(slot, t):
+        rf_s[...] = right_all[slot, pl.ds(t * ch, ch)].astype(F32)
 
         @pl.loop(0, rows // ig)
         def _(ip):
-            accs = [None] * (ig * rows)
+            accs = [None] * (ig * ch)
             for kv in range(cols // 8):
                 ks = slice(kv * 8, kv * 8 + 8)
                 lefts = [left_s[ip * ig + u, ks, :] for u in range(ig)]
-                for j in range(rows):
+                for j in range(ch):
                     rv = rf_s[j, ks, :]
                     for u in range(ig):
-                        n = u * rows + j
+                        n = u * ch + j
                         term = lefts[u] * rv
                         accs[n] = term if accs[n] is None else accs[n] + term
-            for n in range(ig * rows // 8):
-                start = pl.multiple_of(ip * (ig * rows) + n * 8, 8)
-                part_s[slot, pl.ds(start, 8), :] = fold_sublanes(accs[n * 8 : n * 8 + 8])
+            for n in range(ig * ch // 8):
+                start = pl.multiple_of(ip * (ig * ch) + n * 8, 8)
+                part_s[slot, t, pl.ds(start, 8), :] = fold_sublanes(accs[n * 8 : n * 8 + 8])
 
         @pl.when(slot // rb != c)
         def _():
-            part_copy(slot).start()
-
-    def event(n):
-        away = (n + 1) // 2
-        return jnp.where(n % 2 == 1, z - away, z + away)
-
-    @pl.loop(1, 2 * nz)
-    def _(n):
-        zn = event(n)
-
-        @pl.when((zn >= 0) & (zn < nz))
-        def _():
+            part_copy(slot, t).start()
+
+    @pl.loop(0, nt)
+    def _(t):
+        compute(r, t)
+
+    if group == 2:
+        @pl.loop(0, nt)
+        def _(t):
+            right_copy(2, z * group + 1 - p, t).wait_recv()
+            compute(z * group + 1 - p, t)
+
+    steps = nt * (nz - 1)
+
+    @pl.loop(0, steps + (1 if group == 2 else 0))
+    def _(s):
+        away, t = 1 + s // nt, s % nt
+        for below in (True, False):
+            zn = z - away if below else z + away
             slot = zn * group + p
-            for t in range(nt):
+
+            @pl.when((s < steps) & (zn >= 0) & (zn < nz))
+            def _():
                 right_copy(0, slot, t).wait_recv()
-
-                @pl.when((zn < z) & (z + 1 < nz))
-                def _():
-                    right_copy(0, slot, t).start()
-
-                @pl.when((zn > z) & (z >= 1))
-                def _():
-                    right_copy(1, slot, t).start()
-
+                if below:
+                    @pl.when(z + 1 < nz)
+                    def _():
+                        right_copy(0, slot, t).start()
+                else:
+                    @pl.when(z >= 1)
+                    def _():
+                        right_copy(1, slot, t).start()
                 if group == 2:
                     right_copy(2, slot, t).start()
 
-        zp = event(n - 1)
-
-        @pl.when((zp >= 0) & (zp < nz))
-        def _():
-            @pl.loop(0, group)
-            def _(q):
-                slot = zp * group + (p + q) % group
-
-                @pl.when(q == 1)
+        @pl.loop(0, 2 * group)
+        def _(e):
+            old = e // 2
+            sq = s - old
+            awayq, tq = (sq + nt) // nt, (sq + nt) % nt
+            zq = jnp.where(e % 2 == 0, z - awayq, z + awayq)
+            slot = zq * group + (p + old) % group
+
+            @pl.when((sq >= 0) & (sq < steps) & (zq >= 0) & (zq < nz))
+            def _():
+                @pl.when(old == 1)
                 def _():
-                    for t in range(nt):
-                        right_copy(2, slot, t).wait_recv()
-
-                compute(slot)
+                    right_copy(2, slot, tq).wait_recv()
+
+                compute(slot, tq)
 
     for b in range(rb):
-        total = part_s[c * rb + b]
-        for away in range(1, cc):
-            source = (c + away) % cc
-            pltpu.make_async_remote_copy(
-                src_ref=part_s.at[0], dst_ref=part_in.at[source, b],
-                send_sem=ps_send.at[0], recv_sem=ps_recv.at[source, b],
-                device_id=at(r, source), device_id_type=MESH,
-            ).wait_recv()
-            total = total + part_in[source, b]
-        sum_s[b] = total
-        for i in range(rows):
-            tri_s[i, b * rows : (b + 1) * rows, :] = sum_s[b, i * rows : (i + 1) * rows, :]
+        for t in range(nt):
+            total = part_s[c * rb + b, t]
+            for away in range(1, cc):
+                source = (c + away) % cc
+                pltpu.make_async_remote_copy(
+                    src_ref=part_s.at[0, 0], dst_ref=part_in.at[source, b, t],
+                    send_sem=ps_send.at[0, 0], recv_sem=ps_recv.at[source, b, t],
+                    device_id=at(r, source), device_id_type=MESH,
+                ).wait_recv()
+                total = total + part_in[source, b, t]
+            sum_s[b, t] = total
+            first = b * rows + t * ch
+            for i in range(rows):
+                tri_s[i, first : first + ch, :] = sum_s[b, t, i * ch : (i + 1) * ch, :]
 
     def att_copy(t, away, source):
         piece = att_all.at[source, pl.ds(t * ch, ch)]
@@ -235,12 +246,14 @@
         mid_s[t] = mid
         att = norm_last(mid, g3_ref[...]).astype(BF16)
         att_all[c, sl] = att.reshape(ch, cols, chan)
-        for away in range(1, cc):
-            att_copy(t, away, c).start()
+        if t < nt - 1:
+            for away in range(1, cc):
+                att_copy(t, away, c).start()
         for u in range(ch):
             heads_first = dot_nt(w_bias_ref[...], att[u * cols : (u + 1) * cols])
             for h in range(heads):
-                bias_f[h, t * ch + u : t * ch + u + 1, :] = heads_first[h : h + 1, :]
+                at_lane = h % 2 * cols
+                bias_f[h // 2, t * ch + u : t * ch + u + 1, at_lane : at_lane + cols] = heads_first[h : h + 1, :]
 
     bias_own[...] = bias_f[...].astype(BF16)
     panel = r // rb
@@ -252,13 +265,16 @@
             device_id=at(row, panel), device_id_type=MESH,
         )
 
-    @pl.loop(0, nrow)
+    @pl.loop(0, nz)
     def _(n):
-        row = (r + n) % nrow
+        row = (z + n) % nz * group + p
 
         @pl.when((n > 0) | (panel != c))
         def _():
             bias_copy(row, c, r % rb).start()
+
+    for away in range(1, cc):
+        att_copy(nt - 1, away, c).start()
 
     @pl.when(panel == c)
     def _():
@@ -272,6 +288,24 @@
         k_s[c, sl] = proj[:, hid : 2 * hid].astype(BF16).reshape(ch, cols, hid)
         v_s[c, sl] = proj[:, 2 * hid : 3 * hid].astype(BF16).reshape(ch, cols, hid)
         ag_s[sl] = jax.nn.sigmoid(proj[:, 3 * hid :]).reshape(ch, cols, hid)
+
+    def bias_pass(source, b):
+        return pltpu.make_async_remote_copy(
+            src_ref=bias_all.at[source, b], dst_ref=bias_all.at[source, b],
+            send_sem=bf_send.at[source, b], recv_sem=bs_recv.at[source, b],
+            device_id={"row": z * group + (group - 1 - p)}, device_id_type=MESH,
+        )
+
+    for source in range(cc):
+        for b in range(rb):
+            @pl.when((c * rb + b) % group == p)
+            def _():
+                @pl.when((c != source) | (r != c * rb + b))
+                def _():
+                    bias_copy(r, source, b).wait_recv()
+
+                if group == 2:
+                    bias_pass(source, b).start()
 
     for away in range(1, cc):
         source = (c + away) % cc
@@ -286,13 +320,13 @@
     mask_row = (live - 1.0) * mask_penalty
     for source in range(cc):
         for b in range(rb):
-            @pl.when((c != source) | (r != c * rb + b))
+            @pl.when((c * rb + b) % group != p)
             def _():
                 bias_copy(r, source, b).wait_recv()
 
             for h in range(heads):
                 bfull[h, b * rows : (b + 1) * rows, source * cols : (source + 1) * cols] = (
-                    bias_all[source, b, h].astype(F32)[:rows] + mask_row[:, source * cols : (source + 1) * cols]
+                    bias_all[source, b, h // 2].astype(F32)[:rows, h % 2 * cols : (h % 2 + 1) * cols] + mask_row[:, source * cols : (source + 1) * cols]
                 )
 
     head_of = lax.broadcasted_iota(jnp.int32, (cols, hid), 1) // head_size
@@ -341,11 +375,19 @@
 
         @pl.when(slot // rb != c)
         def _():
-            part_copy(slot).wait_send()
-
-        @pl.when((slot != r) | (panel != c))
+            for t in range(nt):
+                part_copy(slot, t).wait_send()
+
+        @pl.when((pn == p) & ((slot != r) | (panel != c)))
         def _():
             bias_copy(slot, c, r % rb).wait_send()
+
+    if group == 2:
+        for source in range(cc):
+            for b in range(rb):
+                @pl.when((c * rb + b) % group == p)
+                def _():
+                    bias_pass(source, b).wait_send()
 
     for away in range(1, cc):
         for t in range(nt):
@@ -377,10 +419,10 @@
             V((nrow, rows, cols, hid), BF16),
             V((rows, cols, hid), F32),
             V((nt, ch * cols, chan), F32),
-            V((rows, cols, hid), F32),
-            V((nrow, rows * rows, hid), F32),
-            V((cc, rb, rows * rows, hid), F32),
-            V((rb, rows * rows, hid), F32),
+            V((ch, cols, hid), F32),
+            V((nrow, nt, rows * ch, hid), F32),
+            V((cc, rb, nt, rows * ch, hid), F32),
+            V((rb, nt, rows * ch, hid), F32),
             V((rows, cols, hid), F32),
             V((nt, ch * cols, chan), F32),
             V((cc, rows, cols, chan), BF16),
@@ -388,17 +430,18 @@
             V((rows, cols, hid), F32),
             V((cc, rows, cols, hid), BF16),
             V((cc, rows, cols, hid), BF16),
-            V((heads, pad, cols), F32),
-            V((heads, pad, cols), BF16),
-            V((cc, rb, heads, pad, cols), BF16),
+            V((heads // 2, pad, 2 * cols), F32),
+            V((heads // 2, pad, 2 * cols), BF16),
+            V((cc, rb, heads // 2, pad, 2 * cols), BF16),
             V((heads, cols, residues), F32),
             DMA((3, nrow, nt)),
             DMA((nrow, nt)),
-            DMA((nrow,)),
-            DMA((cc, rb)),
+            DMA((nrow, nt)),
+            DMA((cc, rb, nt)),
             DMA((cc, nt)),
             DMA((cc, nt)),
             DMA((nrow,)),
+            DMA((cc, rb)),
             DMA((cc, rb)),
         ],
         compiler_params=pltpu.CompilerParams(

time: 43.6 us -> 39.4 us (0.904)
  Pallas kernels: 38.8 us -> 34.5 us
    pallas_call x1, Pallas kernels: 38.8 us -> 34.5 us  [body(): pl.pallas_call(functools.partial(kernel, dims), out_shape=jax.ShapeDtypeS...]
where the time goes in v2:
time: 39.4 us; the launch traced here: 39.2 us
  Pallas kernels  34.5 us (88%)
  local copies, waits for them, and re-layouts  4.65 us (12%)
    pallas_call x1, Pallas kernels, body(): pl.pallas_call(functools.partial(kernel, dims), out_shape=jax.ShapeDtypeS...  34.5 us
    unnamed x3, local copies, waits for them, and re-layouts  2.37 us
    reshape x1, local copies, waits for them, and re-layouts, body(): w_att.reshape(chan, -1)  1.69 us

profile of v2, /device:TPU:0, one launch (start us, length us, event | category | flops | bytes accessed | tf_op | source)
XLA Modules:
  0.0 39.2 jit_solution(6786169705755790303)
XLA Ops:
  0.0 0.0 copy-start
  0.0 0.7 %copy-done = bf16[128,4]{0,1:T(4,128)(2,1)S(1)} copy-done((bf16[128,4]{0,1:T(4,128)(2,1)S(1)}, bf16[128,4]{0,1:T(4,128)(2,1)}, u32[]{:S(2)}) %copy-start) | copy-done | bytes 1048
  0.7 0.6 %pad.4.w_bias_ref = bf16[16,128]{1,0:T(8,128)(2,1)} pad(bf16[4,128]{1,0:T(4,128)(2,1)S(1)} %bitcast.13, bf16[]{:T(256)} %constant.2.clone.1), padding=0_12x0_0 | pad | bytes 5122 | tf_op jit(solution)/shard_map/jit(_pad)/pad | solution.py:408
  1.3 1.7 %copy_bitcast_fusion = (bf16[128,512]{1,0:T(8,128)(2,1)}, bf16[128,512]{1,0:T(8,128)(2,1)}) fusion(bf16[16,8,4,128]{3,2,1,0:T(4,128)(2,1)} %bitcast.11, bf16[16,8,4,128]{3,2,1,0:T(4,128)(2,1)} %bitcast.12), kind=kLoop, calls=%fused_computation | loop fusion | bytes 524288 | tf_op jit(solution)/shard_map/reshape | solution.py:460
  3.0 34.5 %pair_update.1 = f32[12,48,128]{2,1,0:T(8,128)} custom-call(f32[12,48,128]{2,1,0:T(8,128)} %pair_ref.1, s32[1,96]{1,0:T(1,128)} %bitcast.14, f32[1,128]{1,0:T(1,128)} %bitcast.15, bf16[128,512]{1,0:T(8,128)(2,1)} %get-tuple-element.6.w_in_ref, bf16[128,128]{1,0:T(8,128)(2,1)} %w_gate_ref.1, f32[1,128]{1,0:T(1,128)} %bitcast.16, bf16[128,128]{1,0:T(8,128)(2,1)} %w_out_ref.1, ...), custom_call_target="tpu_custom_call" | custom-call | tf_op jit(solution)/shard_map/pair_update/pallas_call | solution.py:411
  37.5 1.7 %copy.17 = f32[12,48,128]{2,1,0:T(8,128)} copy(f32[12,48,128]{2,1,0:T(8,128)} %pair_update.1) | data formatting | bytes 589824
Async XLA Ops:
  0.0 0.7 %copy-start = (bf16[128,4]{0,1:T(4,128)(2,1)S(1)}, bf16[128,4]{0,1:T(4,128)(2,1)}, u32[]{:S(2)}) copy-start(bf16[128,4]{0,1:T(4,128)(2,1)} %param.20) | copy-start | bytes 3076

commit v3 on v2

--- a/solution.py
+++ b/solution.py
@@ -51,11 +51,11 @@
 
 def kernel(
     dims,
-    pair_ref, mask_ref, g1_ref, w_in_ref, w_gate_ref, g2_ref, w_out_ref, g3_ref, w_att_ref, w_bias_ref, w_o_ref,
+    pair_ref, mask_ref, g1_ref, w_in3_ref, w_gate_ref, g2_ref, w_out_ref, g3_ref, w_att3_ref, w_bias_ref, w_o_ref,
     out_ref,
     live_s, normed_s, right_all, left_s, gate_s, rf_s, part_s, part_in, sum_s, tri_s, mid_s,
     att_all, q_s, ag_s, k_s, v_s, bias_f, bias_own, bias_all, bfull,
-    rs_send, rs_recv, ps_send, ps_recv, as_send, as_recv, bs_send, bs_recv, bf_send,
+    rs_send, rs_recv, ps_send, ps_recv, as_send, as_recv, bs_send, bs_recv, bf_send, w_in_ref, w_att_ref, wide_s,
 ):
     nrow, ncol, nsub, group = dims
     rows, cols, chan = pair_ref.shape
@@ -77,6 +77,12 @@
     def at(row, cc_index):
         return {"row": row, "col": cc_index // nsub, "sub": cc_index % nsub}
 
+    def spread(w_ref, flat_ref):
+        for n in range(chan):
+            wide_s[n * 4 : n * 4 + 4, :] = w_ref[n].astype(F32)
+        for n in range(4):
+            flat_ref[:, n * hid : (n + 1) * hid] = wide_s[pl.ds(n, chan, stride=4), :].astype(BF16)
+
     barrier = pltpu.get_barrier_semaphore()
     me = r * cc + c
 
@@ -84,6 +90,8 @@
     def _(n):
         other = (me + n) % (nrow * cc)
         pl.semaphore_signal(barrier, inc=1, device_id=at(other // cc, other % cc), device_id_type=MESH)
+
+    spread(w_in3_ref, w_in_ref)
 
     live = mask_ref[...].astype(F32)
     eye = lax.broadcasted_iota(jnp.int32, (residues, residues), 0) == lax.broadcasted_iota(
@@ -140,6 +148,7 @@
             device_id=at(r, slot // rb), device_id_type=MESH,
         )
 
+    spread(w_att3_ref, w_att_ref)
     ig = next(n for n in (4, 2, 1) if rows % n == 0 and n * ch % 8 == 0)
 
     def compute(slot, t):
@@ -405,7 +414,6 @@
     ch = next(n for n in (4, 2, 1) if rows % n == 0)
     nt = rows // ch
     pad = -(-rows // 16) * 16
-    bias_rows = jnp.pad(w_bias.T, ((0, -heads % 16), (0, 0)))
     V = pltpu.VMEM
     DMA = pltpu.SemaphoreType.DMA
     return pl.pallas_call(
@@ -443,6 +451,9 @@
             DMA((nrow,)),
             DMA((cc, rb)),
             DMA((cc, rb)),
+            V((chan, 4 * hid), BF16),
+            V((chan, 4 * hid), BF16),
+            V((4 * chan, hid), F32),
         ],
         compiler_params=pltpu.CompilerParams(
             collective_id=0, has_side_effects=True, vmem_limit_bytes=56 * 1024 * 1024
@@ -452,13 +463,13 @@
         pair,
         residue_mask.reshape(1, -1),
         g1.reshape(1, -1),
-        w_in.reshape(chan, -1),
+        w_in,
         w_gate,
         g2.reshape(1, -1),
         w_out,
         g3.reshape(1, -1),
-        w_att.reshape(chan, -1),
-        bias_rows,
+        w_att,
+        w_bias.T,
         w_o,
     )
 

time: 39.4 us -> 36.4 us (0.924)
  local copies, waits for them, and re-layouts: 4.65 us -> 1.69 us
    reshape x1 -> x0, local copies, waits for them, and re-layouts: 1.69 us -> none  [body(): w_att.reshape(chan, -1)]
    unnamed x3 -> x1, local copies, waits for them, and re-layouts: 2.37 us -> 1.69 us
    pad x1 -> x0, local copies, waits for them, and re-layouts: 0.59 us -> none  [body(): bias_rows = jnp.pad(w_bias.T, ((0, -heads % 16), (0, 0)))]
where the time goes in v3:
time: 36.4 us; the launch traced here: 36.2 us
  Pallas kernels  34.5 us (95%)
  local copies, waits for them, and re-layouts  1.69 us (5%)
    pallas_call x1, Pallas kernels, body(): pl.pallas_call(functools.partial(kernel, dims), out_shape=jax.ShapeDtypeS...  34.5 us
    unnamed x1, local copies, waits for them, and re-layouts  1.69 us

profile of v3, /device:TPU:0, one launch (start us, length us, event | category | flops | bytes accessed | tf_op | source)
XLA Modules:
  0.0 36.2 jit_solution(6966020740839560272)
XLA Ops:
  0.0 34.5 %pair_update.1 = f32[12,48,128]{2,1,0:T(8,128)} custom-call(f32[12,48,128]{2,1,0:T(8,128)} %pair_ref.1, s32[1,96]{1,0:T(1,128)} %bitcast.6, f32[1,128]{1,0:T(1,128)} %bitcast.7, bf16[128,4,128]{2,1,0:T(4,128)(2,1)} %w_in3_ref.1, bf16[128,128]{1,0:T(8,128)(2,1)} %w_gate_ref.1, f32[1,128]{1,0:T(1,128)} %bitcast.8, bf16[128,128]{1,0:T(8,128)(2,1)} %w_out_ref.1, ...), custom_call_target="tpu_custom_call" | custom-call | tf_op jit(solution)/shard_map/pair_update/pallas_call | solution.py:419
  34.6 1.7 %copy.13 = f32[12,48,128]{2,1,0:T(8,128)} copy(f32[12,48,128]{2,1,0:T(8,128)} %pair_update.1) | data formatting | bytes 589824
